TPU v7x, 32 devices: a whole 2x2x4 slice. The times are simulated.
32 devices in a mesh: ta: 16 (over z, x, core), aa: 2 (over y).
Axes of the slice: x: 2, y: 2, z: 4, core: 2. Of those that a mesh axis runs over, the one named last changes fastest.
Arguments:
- voltages: bfloat16 [256, 393216], P('aa', 'ta'), may hold values from -6 to 6
- pfb_window: float32 [4, 8192], replicated, may hold values from -3 to 3
Outputs:
- visibilities: float32 [2048, 256, 512], P('ta', 'aa')
All inputs are finite; a program needn't handle non-finite values.
Results may differ from a plain program's by a relative error of at most 0.0026.
Values may be sent and summed in bfloat16 or wider, within the bound.
A program may use at most 192 MiB of HBM per device.

v0:
```python
import functools
import math

import jax
import jax.numpy as jnp
import numpy as np
from jax import lax
from jax.experimental import pallas as pl
from jax.experimental.pallas import tpu as pltpu
from jax.sharding import PartitionSpec as P


NFFT = 8192
CH = 2048
TAPS = 4
CH_OFF = 1024
RADIX = 32
INNER = NFFT // RADIX
BINS = CH // RADIX
HALF = RADIX // 2
LANES = 128
SIG_BLOCK = 16


def split_bf16(x):
    hi = jnp.asarray(x, jnp.bfloat16)
    return hi, (x - hi.astype(jnp.float32)).astype(jnp.bfloat16)


def stage_two_matrix():
    n2 = np.arange(INNER)[None, :]
    m = np.arange(BINS)[:, None] + CH_OFF // RADIX
    angle = 2.0 * np.pi * ((n2 * m) % INNER) / INNER
    mirror = 2.0 * np.pi * ((n2 * (m + 1)) % INNER) / INNER
    rows = [
        np.concatenate([np.cos(angle), np.sin(angle)], axis=1),
        np.concatenate([-np.sin(angle), np.cos(angle)], axis=1),
        np.concatenate([np.cos(mirror), -np.sin(mirror)], axis=1),
        np.concatenate([-np.sin(mirror), -np.cos(mirror)], axis=1),
    ]
    full = np.concatenate(rows, axis=0) / math.sqrt(NFFT)
    hi = full.astype(jnp.bfloat16)
    lo = (full - hi.astype(np.float64)).astype(jnp.bfloat16)
    return hi, lo


def twist_table():
    k = np.arange(HALF + 1)[:, None]
    n2 = np.arange(INNER)[None, :]
    angle = 2.0 * np.pi * (k * n2) / NFFT
    return np.stack([np.cos(angle), -np.sin(angle)]).astype(np.float32)


def rfft_list(x):
    n = len(x)
    if n == 2:
        return [(x[0] + x[1], None), (x[0] - x[1], None)]
    even, odd = rfft_list(x[0::2]), rfft_list(x[1::2])
    out = [None] * (n // 2 + 1)
    for k in range(n // 4 + 1):
        er, ei = even[k]
        our, oui = odd[k]
        if k == 0:
            out[0] = (er + our, None)
            out[n // 2] = (er - our, None)
        elif k == n // 4:
            out[k] = (er, -our)
        else:
            c = math.cos(2 * math.pi * k / n)
            s = math.sin(2 * math.pi * k / n)
            if 8 * k == n:
                tr, ti = (our + oui) * c, (oui - our) * c
            else:
                tr, ti = our * c + oui * s, oui * c - our * s
            out[k] = (er + tr, ei + ti)
            out[n // 2 - k] = (er - tr, ti - ei)
    return out


def channel_kernel(steps, signals, *refs):
    taps = refs[:TAPS]
    win, twist, mat_hi, mat_lo, out, parts_s, spec_s = refs[TAPS:]
    step = pl.program_id(0)
    rows = pl.ds(pl.multiple_of(step * SIG_BLOCK, SIG_BLOCK), SIG_BLOCK)
    low_rows = pl.ds(pl.multiple_of(signals + step * SIG_BLOCK, SIG_BLOCK), SIG_BLOCK)

    for part in range(INNER // LANES):
        filtered = []
        for n1 in range(RADIX):
            cols = pl.ds(n1 * INNER + part * LANES, LANES)
            total = win[0:1, cols] * taps[0][:, cols].astype(jnp.float32)
            for t in range(1, TAPS):
                total = total + win[t : t + 1, cols] * taps[t][:, cols].astype(jnp.float32)
            filtered.append(total)
        here = pl.ds(part * LANES, LANES)
        there = pl.ds(INNER + part * LANES, LANES)
        for k, (ar, ai) in enumerate(rfft_list(filtered)):
            if k == 0:
                br, bi = ar, jnp.zeros_like(ar)
            else:
                tr, ti = twist[0, k : k + 1, here], twist[1, k : k + 1, here]
                if ai is None:
                    br, bi = ar * tr, ar * ti
                else:
                    br, bi = ar * tr - ai * ti, ar * ti + ai * tr
            for value, cols in ((br, here), (bi, there)):
                hi, lo = split_bf16(value)
                parts_s[k, rows, cols] = hi
                parts_s[k, low_rows, cols] = lo

    @pl.when(step == steps - 1)
    def _():
        dims = (((1,), (1,)), ((), ()))

        def dot(a, b):
            return lax.dot_general(a, b, dims, preferred_element_type=jnp.float32)

        def put(value, k):
            spec_s[0, pl.ds(k, BINS, stride=RADIX), :] = value[:BINS]
            spec_s[1, pl.ds(k, BINS, stride=RADIX), :] = value[BINS:]

        for k in range(HALF + 1):
            size = 2 * BINS if k in (0, HALF) else 4 * BINS
            a_hi, a_lo = mat_hi[:size, :], mat_lo[:size, :]
            both = dot(a_hi, parts_s[k])
            small = dot(a_lo, parts_s[k, :signals])
            res = both[:, :signals] + (both[:, signals:] + small)
            put(res[: 2 * BINS], k)
            if size > 2 * BINS:
                put(res[2 * BINS :], RADIX - k)

        def cast(i, carry):
            at = pl.ds(pl.multiple_of(i * 64, 64), 64)
            out[at, :signals] = spec_s[0, at, :].astype(jnp.bfloat16)
            out[at, signals:] = spec_s[1, at, :].astype(jnp.bfloat16)
            return carry

        lax.fori_loop(0, CH // 64, cast, 0)


def channelize(pieces, window, signals):
    steps = signals // SIG_BLOCK
    mat_hi, mat_lo = stage_two_matrix()

    def tap_spec(frame):
        return pl.BlockSpec((SIG_BLOCK, NFFT), lambda i, frame=frame: (i, frame))

    whole = lambda shape: pl.BlockSpec(shape, lambda i: (0,) * len(shape))
    return pl.pallas_call(
        functools.partial(channel_kernel, steps, signals),
        grid=(steps,),
        out_shape=jax.ShapeDtypeStruct((CH, 2 * signals), jnp.bfloat16),
        in_specs=[tap_spec(frame) for _, frame in pieces]
        + [
            whole((TAPS, NFFT)),
            whole((2, HALF + 1, INNER)),
            whole((4 * BINS, 2 * INNER)),
            whole((4 * BINS, 2 * INNER)),
        ],
        out_specs=whole((CH, 2 * signals)),
        scratch_shapes=[
            pltpu.VMEM((HALF + 1, 2 * signals, 2 * INNER), jnp.bfloat16),
            pltpu.VMEM((2, CH, signals), jnp.float32),
        ],
        compiler_params=pltpu.CompilerParams(
            dimension_semantics=("arbitrary",), vmem_limit_bytes=48 * 1024 * 1024
        ),
        cost_estimate=pl.CostEstimate(
            flops=8_000_000_000, bytes_accessed=10_000_000, transcendentals=0
        ),
    )(
        *[piece for piece, _ in pieces],
        window,
        jnp.asarray(twist_table()),
        jnp.asarray(mat_hi),
        jnp.asarray(mat_lo),
    )


def correlate_kernel(chunks, signals, block, scale, *refs):
    mine = refs[1 : 1 + chunks]
    far = refs[1 + chunks : 1 + 2 * chunks]
    out = refs[-1]
    dims = (((0,), (0,)), ((), ()))

    def write(right_of):
        for c in range(block):
            left = [r[c, :, :signals] for r in mine] + [r[c, :, signals:] for r in mine]
            out[c] = lax.dot_general(
                jnp.concatenate(left, axis=0), jnp.concatenate(right_of(c), axis=0), dims,
                preferred_element_type=jnp.float32) * scale

    @pl.when(pl.program_id(1) == 0)
    def _():
        write(lambda c: [r[c, :, :signals] for r in far] + [r[c, :, signals:] for r in far])

    @pl.when(pl.program_id(1) == 1)
    def _():
        write(lambda c: [-r[c, :, signals:] for r in far] + [r[c, :, :signals] for r in far])


def correlate(mine, far, place, scale, signals, partial=None):
    channels, peers, _ = mine[0].shape
    block = 16 if channels % 16 == 0 and peers <= 32 else 8
    spec = pl.BlockSpec((block, peers, 2 * signals), lambda i, h, p: (i, 0, 0))
    extra = [] if partial is None else [partial]
    count = 2 * len(mine)
    return pl.pallas_call(
        functools.partial(correlate_kernel, len(mine), signals, block, scale),
        grid_spec=pltpu.PrefetchScalarGridSpec(
            num_scalar_prefetch=1,
            grid=(channels // block, 2),
            in_specs=[spec] * count + [pl.BlockSpec(memory_space=pl.ANY)] * len(extra),
            out_specs=pl.BlockSpec(
                (block, signals, signals), lambda i, h, p: (i, 0, 2 * h + p[0])),
        ),
        out_shape=jax.ShapeDtypeStruct((channels, signals, 4 * signals), jnp.float32),
        input_output_aliases={1 + count: 0} if extra else {},
        compiler_params=pltpu.CompilerParams(
            dimension_semantics=("arbitrary", "arbitrary"), vmem_limit_bytes=40 * 1024 * 1024
        ),
        cost_estimate=pl.CostEstimate(
            flops=2_000_000_000, bytes_accessed=24_000_000, transcendentals=0
        ),
    )(place.astype(jnp.int32).reshape(1), *mine, *far, *extra)


def per_device(voltages, pfb_window):
    signals, samples = voltages.shape
    frames = samples // NFFT
    peers = lax.axis_size("ta")
    sides = lax.axis_size("aa")
    assert sides == 2 and frames >= TAPS - 1 and signals % LANES == 0
    onward = [(i, i + 1) for i in range(peers - 1)]
    across = [(i, 1 - i) for i in range(sides)]

    history = {}
    for frame in range(frames - 1, frames - TAPS, -1):
        tail = voltages[:, frame * NFFT : (frame + 1) * NFFT]
        history[frame - frames] = lax.ppermute(tail, "ta", onward)

    own, other, spectra = {}, {}, None

    def swap(frame, spectra_or_owned):
        owned = jnp.transpose(spectra_or_owned, (1, 0, 2))
        own[frame] = owned
        other[frame] = lax.ppermute(owned, "aa", across)

    turned = {}
    for frame in range(frames - 1, -1, -1):
        at_needed = frame - (TAPS - 1)
        if spectra is not None and at_needed < 0:
            held = (history[at_needed], spectra)
            if frame + 2 in turned:
                history[at_needed], _, turned[frame + 2] = lax.optimization_barrier(
                    held + (turned[frame + 2],))
            else:
                history[at_needed], _ = lax.optimization_barrier(held)
        if frame + 2 in turned:
            swap(frame + 2, turned.pop(frame + 2))
        pieces = []
        for tap in range(TAPS):
            at = frame - (TAPS - 1) + tap
            pieces.append((voltages, at) if at >= 0 else (history[at], 0))
        spectra = channelize(pieces, pfb_window, signals)
        if frame == 0:
            for late in sorted(turned, reverse=True):
                turned[late], spectra = lax.optimization_barrier((turned[late], spectra))
                swap(late, turned.pop(late))
        turned[frame] = lax.all_to_all(
            spectra.reshape(peers, CH // peers, 2 * signals), "ta",
            split_axis=0, concat_axis=0, tiled=True)
    for late in sorted(turned, reverse=True):
        swap(late, turned.pop(late))

    order = sorted(own)
    mine = [own[f] for f in order]
    scale = 1.0 / math.sqrt(frames * peers)
    side = lax.axis_index("aa")
    near = correlate(mine, mine, side, scale, signals)
    return correlate(mine, [other[f] for f in order], 1 - side, scale, signals, near)


def solution(mesh):
    in_specs = (P("aa", "ta"), P())
    out_specs = P("ta", "aa", None)
    return jax.shard_map(
        per_device, mesh=mesh, in_specs=in_specs, out_specs=out_specs, check_vma=False
    )
```

profile of v0, /device:TPU:0, one launch (start us, length us, event | category | flops | bytes accessed | tf_op | source)
XLA Modules:
  0.0 224.8 jit_solution(8183059601218278308)
XLA Ops:
  0.0 5.7 %fusion = (bf16[128,8192]{1,0:T(8,128)(2,1)}, bf16[128,8192]{1,0:T(8,128)(2,1)S(1)}, bf16[128,8192]{1,0:T(8,128)(2,1)}) fusion(bf16[128,24576]{1,0:T(8,128)(2,1)} %refs_3_.5), kind=kLoop, calls=%fused_computation.3 | loop fusion | bytes 12582912 | tf_op jit(solution)/shard_map/slice | solution.py:239
  5.7 2.5 %collective-permute-start.1 = (bf16[128,8192]{1,0:T(8,128)(2,1)S(1)}, bf16[128,8192]{1,0:T(8,128)(2,1)S(1)}, u32[]{:S(2)}, u32[]{:S(2)}) collective-permute-start(bf16[128,8192]{1,0:T(8,128)(2,1)S(1)} %get-tuple-element.16), channel_id=1, source_target_pairs={{0,2},{2,4},{4,6},{6,8},{8,10},{10,12},{12,14},{14,16},{16,18},{18... | collective-permute-start | bytes 6291464 | tf_op jit(solution)/shard_map/ppermute | solution.py:240
  8.2 5.7 %collective-permute-start = (bf16[128,8192]{1,0:T(8,128)(2,1)}, bf16[128,8192]{1,0:T(8,128)(2,1)}, u32[]{:S(2)}, u32[]{:S(2)}) collective-permute-start(bf16[128,8192]{1,0:T(8,128)(2,1)} %get-tuple-element.17), channel_id=1, source_target_pairs={{0,2},{2,4},{4,6},{6,8},{8,10},{10,12},{12,14},{14,16},{16,18},{18... | collective-permute-start | bytes 6291464 | tf_op jit(solution)/shard_map/ppermute | solution.py:240
  13.9 0.0 collective-permute-done.1.refs_0_.refs_1_.refs_2_
  14.0 12.4 %shard_map.109 = bf16[2048,256]{1,0:T(8,128)(2,1)} custom-call(bf16[128,8192]{1,0:T(8,128)(2,1)S(1)} %collective-permute-done.1.refs_0_.refs_1_.refs_2_, bf16[128,24576]{1,0:T(8,128)(2,1)} %refs_3_.5, bf16[128,24576]{1,0:T(8,128)(2,1)} %refs_3_.5, bf16[128,24576]{1,0:T(8,128)(2,1)} %refs_3_.5, f32[4,8192]{1,0:T(4,128)S(1)} %copy-done.1, ...), custom_call_target="tpu_custom_call" | custom-call | flops 8000000000 | bytes 10000000 | tf_op jit(solution)/shard_map/pallas_call | solution.py:149
  26.4 26.5 %all-to-all-start.1 = ((bf16[16,128,256]{2,1,0:T(8,128)(2,1)}), bf16[16,128,256]{2,1,0:T(8,128)(2,1)}, u32[]{:S(2)}, u32[]{:S(2)}) async-start(bf16[16,128,256]{2,1,0:T(8,128)(2,1)} %bitcast.2), calls=%async_computation.1 | async-start | bytes 2097152 | tf_op jit(solution)/shard_map/all_to_all | solution.py:270
  52.9 3.6 %collective-permute-start.2 = (bf16[128,8192]{1,0:T(8,128)(2,1)}, bf16[128,8192]{1,0:T(8,128)(2,1)}, u32[]{:S(2)}, u32[]{:S(2)}) collective-permute-start(bf16[128,8192]{1,0:T(8,128)(2,1)} %get-tuple-element.15), channel_id=1, source_target_pairs={{0,2},{2,4},{4,6},{6,8},{8,10},{10,12},{12,14},{14,16},{16,18},{18... | collective-permute-start | bytes 6291464 | tf_op jit(solution)/shard_map/ppermute | solution.py:240
  56.5 11.8 %shard_map.110 = bf16[2048,256]{1,0:T(8,128)(2,1)} custom-call(bf16[128,8192]{1,0:T(8,128)(2,1)} %collective-permute-done.refs_0_.refs_1_, bf16[128,8192]{1,0:T(8,128)(2,1)S(1)} %collective-permute-done.1.refs_0_.refs_1_.refs_2_, bf16[128,24576]{1,0:T(8,128)(2,1)} %refs_3_.5, bf16[128,24576]{1,0:T(8,128)(2,1)} %refs_3_.5, f32[4,8192]{1,0:T(4,128)S(1)} %copy-done.1, ...), custom_call_target="tpu_custom_call" | custom-call | flops 8000000000 | bytes 10000000 | tf_op jit(solution)/shard_map/pallas_call | solution.py:149
  68.4 7.5 %all-to-all-done.1 = bf16[16,128,256]{2,1,0:T(8,128)(2,1)} async-done(((bf16[16,128,256]{2,1,0:T(8,128)(2,1)}), bf16[16,128,256]{2,1,0:T(8,128)(2,1)}, u32[]{:S(2)}, u32[]{:S(2)}) %all-to-all-start.1) | async-done | bytes 1048608 | tf_op jit(solution)/shard_map/all_to_all | solution.py:270
  75.9 8.8 %all-to-all-start = ((bf16[16,128,256]{2,1,0:T(8,128)(2,1)}), bf16[16,128,256]{2,1,0:T(8,128)(2,1)S(1)}, u32[]{:S(2)}, u32[]{:S(2)}) async-start(bf16[16,128,256]{2,1,0:T(8,128)(2,1)} %bitcast.1), calls=%async_computation | async-start | bytes 2097152 | tf_op jit(solution)/shard_map/all_to_all | solution.py:270
  84.6 12.2 %shard_map.111 = bf16[2048,256]{1,0:T(8,128)(2,1)} custom-call(bf16[128,8192]{1,0:T(8,128)(2,1)} %collective-permute-done.2.refs_0_, bf16[128,8192]{1,0:T(8,128)(2,1)} %collective-permute-done.refs_0_.refs_1_, bf16[128,8192]{1,0:T(8,128)(2,1)} %copy-done, bf16[128,24576]{1,0:T(8,128)(2,1)} %refs_3_.5, f32[4,8192]{1,0:T(4,128)S(1)} %copy-done.1, ...), custom_call_target="tpu_custom_call" | custom-call | flops 8000000000 | bytes 10000000 | tf_op jit(solution)/shard_map/pallas_call | solution.py:149
  96.8 10.7 %all-to-all-done = bf16[16,128,256]{2,1,0:T(8,128)(2,1)S(1)} async-done(((bf16[16,128,256]{2,1,0:T(8,128)(2,1)}), bf16[16,128,256]{2,1,0:T(8,128)(2,1)S(1)}, u32[]{:S(2)}, u32[]{:S(2)}) %all-to-all-start) | async-done | bytes 1048608 | tf_op jit(solution)/shard_map/all_to_all | solution.py:270
  107.5 28.5 %all-to-all-start.2 = ((bf16[16,128,256]{2,1,0:T(8,128)(2,1)}), bf16[16,128,256]{2,1,0:T(8,128)(2,1)}, u32[]{:S(2)}, u32[]{:S(2)}) async-start(bf16[16,128,256]{2,1,0:T(8,128)(2,1)} %bitcast.3), calls=%async_computation.2 | async-start | bytes 2097152 | tf_op jit(solution)/shard_map/all_to_all | solution.py:270
  136.0 0.6 copy.23
  136.6 1.8 copy.22
  138.4 1.6 collective-permute-start.5
  140.0 0.5 collective-permute-start.4
  140.5 18.4 %all-to-all-done.2 = bf16[16,128,256]{2,1,0:T(8,128)(2,1)} async-done(((bf16[16,128,256]{2,1,0:T(8,128)(2,1)}), bf16[16,128,256]{2,1,0:T(8,128)(2,1)}, u32[]{:S(2)}, u32[]{:S(2)}) %all-to-all-start.2) | async-done | bytes 1048608 | tf_op jit(solution)/shard_map/all_to_all | solution.py:270
  158.9 1.8 copy.24
  160.7 1.6 collective-permute-start.3
  162.3 10.9 %shard_map.112.refs_7_ = f32[128,128,512]{2,1,0:T(8,128)} custom-call(s32[1]{0:T(128)} %bitcast.7.refs_0_, bf16[128,16,256]{2,1,0:T(8,128)(2,1)S(1)} %bitcast.23, bf16[128,16,256]{2,1,0:T(8,128)(2,1)S(1)} %bitcast.15, bf16[128,16,256]{2,1,0:T(8,128)(2,1)S(1)} %bitcast.19, bf16[128,16,256]{2,1,0:T(8,128)(2,1)S(1)} %bitcast.24, ...), custom_call_target="tpu_custom_call" | custom-call | flops 2000000000 | bytes 24000000 | tf_op jit(solution)/shard_map/pallas_call | solution.py:208
  173.2 13.8 %collective-permute-done.4.refs_5_ = bf16[128,16,256]{2,1,0:T(8,128)(2,1)} collective-permute-done((bf16[128,16,256]{2,1,0:T(8,128)(2,1)S(1)}, bf16[128,16,256]{2,1,0:T(8,128)(2,1)}, u32[]{:S(2)}, u32[]{:S(2)}) %collective-permute-start.4) | collective-permute-done | bytes 1048608 | tf_op jit(solution)/shard_map/ppermute | solution.py:247
  187.1 21.8 %collective-permute-done.3.refs_4_ = bf16[128,16,256]{2,1,0:T(8,128)(2,1)} collective-permute-done((bf16[128,16,256]{2,1,0:T(8,128)(2,1)S(1)}, bf16[128,16,256]{2,1,0:T(8,128)(2,1)}, u32[]{:S(2)}, u32[]{:S(2)}) %collective-permute-start.3) | collective-permute-done | bytes 1048608 | tf_op jit(solution)/shard_map/ppermute | solution.py:247
  208.9 15.9 %shard_map.113 = f32[128,128,512]{2,1,0:T(8,128)} custom-call(s32[1]{0:T(128)} %bitcast.refs_0_, bf16[128,16,256]{2,1,0:T(8,128)(2,1)S(1)} %bitcast.25, bf16[128,16,256]{2,1,0:T(8,128)(2,1)S(1)} %bitcast.17, bf16[128,16,256]{2,1,0:T(8,128)(2,1)S(1)} %bitcast.21, ...), custom_call_target="tpu_custom_call", output_to_operand_aliasing={{}: (7, {})} | custom-call | flops 2000000000 | bytes 24000000 | tf_op jit(solution)/shard_map/pallas_call | solution.py:208
  (13 shorter events, 0.0 us)
Async XLA Ops:
  0.0 13.9 %copy-start.2 = (bf16[256,512]{1,0:T(8,128)(2,1)S(1)}, bf16[256,512]{1,0:T(8,128)(2,1)}, u32[]{:S(2)}) copy-start(bf16[256,512]{1,0:T(8,128)(2,1)} %constant.14.clone.refs_7_) | copy-start | bytes 786436
  0.0 13.9 %copy-start.3 = (bf16[256,512]{1,0:T(8,128)(2,1)S(1)}, bf16[256,512]{1,0:T(8,128)(2,1)}, u32[]{:S(2)}) copy-start(bf16[256,512]{1,0:T(8,128)(2,1)} %constant.13.clone.refs_6_) | copy-start | bytes 786436
  0.0 13.9 %copy-start.4 = (f32[2,17,256]{2,1,0:T(8,128)S(1)}, f32[2,17,256]{2,1,0:T(8,128)}, u32[]{:S(2)}) copy-start(f32[2,17,256]{2,1,0:T(8,128)} %constant.12.clone.refs_5_) | copy-start | bytes 104452
  0.0 13.9 %copy-start.1 = (f32[4,8192]{1,0:T(4,128)S(1)}, f32[4,8192]{1,0:T(4,128)}, u32[]{:S(2)}) copy-start(f32[4,8192]{1,0:T(4,128)} %refs_4_.5) | copy-start | bytes 393220
  5.7 8.3 %collective-permute-start.1 = (bf16[128,8192]{1,0:T(8,128)(2,1)S(1)}, bf16[128,8192]{1,0:T(8,128)(2,1)S(1)}, u32[]{:S(2)}, u32[]{:S(2)}) collective-permute-start(bf16[128,8192]{1,0:T(8,128)(2,1)S(1)} %get-tuple-element.16), channel_id=1, source_target_pairs={{0,2},{2,4},{4,6},{6,8},{8,10},{10,12},{12,14},{14,16},{16,18},{18... | collective-permute-start | bytes 6291464 | tf_op jit(solution)/shard_map/ppermute | solution.py:240
  8.2 48.3 %collective-permute-start = (bf16[128,8192]{1,0:T(8,128)(2,1)}, bf16[128,8192]{1,0:T(8,128)(2,1)}, u32[]{:S(2)}, u32[]{:S(2)}) collective-permute-start(bf16[128,8192]{1,0:T(8,128)(2,1)} %get-tuple-element.17), channel_id=1, source_target_pairs={{0,2},{2,4},{4,6},{6,8},{8,10},{10,12},{12,14},{14,16},{16,18},{18... | collective-permute-start | bytes 6291464 | tf_op jit(solution)/shard_map/ppermute | solution.py:240
  14.0 42.6 %copy-start = (bf16[128,8192]{1,0:T(8,128)(2,1)}, bf16[128,8192]{1,0:T(8,128)(2,1)S(1)}, u32[]{:S(2)}) copy-start(bf16[128,8192]{1,0:T(8,128)(2,1)S(1)} %collective-permute-done.1.refs_0_.refs_1_.refs_2_) | copy-start | bytes 6291460
  26.4 49.5 %all-to-all-start.1 = ((bf16[16,128,256]{2,1,0:T(8,128)(2,1)}), bf16[16,128,256]{2,1,0:T(8,128)(2,1)}, u32[]{:S(2)}, u32[]{:S(2)}) async-start(bf16[16,128,256]{2,1,0:T(8,128)(2,1)} %bitcast.2), calls=%async_computation.1 | async-start | bytes 2097152 | tf_op jit(solution)/shard_map/all_to_all | solution.py:270
  52.9 31.7 %collective-permute-start.2 = (bf16[128,8192]{1,0:T(8,128)(2,1)}, bf16[128,8192]{1,0:T(8,128)(2,1)}, u32[]{:S(2)}, u32[]{:S(2)}) collective-permute-start(bf16[128,8192]{1,0:T(8,128)(2,1)} %get-tuple-element.15), channel_id=1, source_target_pairs={{0,2},{2,4},{4,6},{6,8},{8,10},{10,12},{12,14},{14,16},{16,18},{18... | collective-permute-start | bytes 6291464 | tf_op jit(solution)/shard_map/ppermute | solution.py:240
  75.9 31.7 %all-to-all-start = ((bf16[16,128,256]{2,1,0:T(8,128)(2,1)}), bf16[16,128,256]{2,1,0:T(8,128)(2,1)S(1)}, u32[]{:S(2)}, u32[]{:S(2)}) async-start(bf16[16,128,256]{2,1,0:T(8,128)(2,1)} %bitcast.1), calls=%async_computation | async-start | bytes 2097152 | tf_op jit(solution)/shard_map/all_to_all | solution.py:270
  107.5 51.4 %all-to-all-start.2 = ((bf16[16,128,256]{2,1,0:T(8,128)(2,1)}), bf16[16,128,256]{2,1,0:T(8,128)(2,1)}, u32[]{:S(2)}, u32[]{:S(2)}) async-start(bf16[16,128,256]{2,1,0:T(8,128)(2,1)} %bitcast.3), calls=%async_computation.2 | async-start | bytes 2097152 | tf_op jit(solution)/shard_map/all_to_all | solution.py:270
  138.4 34.8 %collective-permute-start.5 = (bf16[128,16,256]{2,1,0:T(8,128)(2,1)S(1)}, bf16[128,16,256]{2,1,0:T(8,128)(2,1)}, u32[]{:S(2)}, u32[]{:S(2)}) collective-permute-start(bf16[128,16,256]{2,1,0:T(8,128)(2,1)S(1)} %bitcast.18), channel_id=1, source_target_pairs={{0,1},{1,0},{2,3},{3,2},{4,5},{5,4},{6,7},{7,6},{8,9},{9,8},{10,11... | collective-permute-start | bytes 3145736 | tf_op jit(solution)/shard_map/ppermute | solution.py:247
  140.0 47.1 %collective-permute-start.4 = (bf16[128,16,256]{2,1,0:T(8,128)(2,1)S(1)}, bf16[128,16,256]{2,1,0:T(8,128)(2,1)}, u32[]{:S(2)}, u32[]{:S(2)}) collective-permute-start(bf16[128,16,256]{2,1,0:T(8,128)(2,1)S(1)} %bitcast.14), channel_id=1, source_target_pairs={{0,1},{1,0},{2,3},{3,2},{4,5},{5,4},{6,7},{7,6},{8,9},{9,8},{10,11... | collective-permute-start | bytes 3145736 | tf_op jit(solution)/shard_map/ppermute | solution.py:247
  160.7 48.2 %collective-permute-start.3 = (bf16[128,16,256]{2,1,0:T(8,128)(2,1)S(1)}, bf16[128,16,256]{2,1,0:T(8,128)(2,1)}, u32[]{:S(2)}, u32[]{:S(2)}) collective-permute-start(bf16[128,16,256]{2,1,0:T(8,128)(2,1)S(1)} %bitcast.22), channel_id=1, source_target_pairs={{0,1},{1,0},{2,3},{3,2},{4,5},{5,4},{6,7},{7,6},{8,9},{9,8},{10,11... | collective-permute-start | bytes 3145736 | tf_op jit(solution)/shard_map/ppermute | solution.py:247
where the time goes:
time: 226 us; the launch traced here: 225 us
  starting transfers between devices  79.3 us (35%)
  waiting for transfers between devices  72.3 us (32%)
  Pallas kernels  63.2 us (28%)
  local copies, waits for them, and re-layouts  9.89 us (4%)
    all_to_all x3, starting transfers between devices, per_device(): lax.all_to_all(spectra.reshape(peers, CH // peers, 2 * signals), 'ta', sp...  63.8 us
    all_to_all x3, waiting for transfers between devices, per_device(): lax.all_to_all(spectra.reshape(peers, CH // peers, 2 * signals), 'ta', sp...  36.6 us
    pallas_call x3, Pallas kernels, channelize(): pl.pallas_call(functools.partial(channel_kernel, steps, signals), grid=(s...  36.4 us
    ppermute x3, waiting for transfers between devices, swap(): other[frame] = lax.ppermute(owned, 'aa', across)  35.7 us
    pallas_call x2, Pallas kernels, correlate(): pl.pallas_call(functools.partial(correlate_kernel, len(mine), signals, bl...  26.8 us
    ppermute x3, starting transfers between devices, per_device(): history[frame - frames] = lax.ppermute(tail, 'ta', onward)  11.9 us
    slice x1, local copies, waits for them, and re-layouts, per_device(): tail = voltages[:, frame * NFFT:(frame + 1) * NFFT]  5.66 us
  transfers between devices with their start and end apart: 9, of which 5 were waited for; matrix products, arithmetic and copies ran while one was open for 2% of the time, Pallas kernels for 21%

commit v1 on v0

--- a/solution.py
+++ b/solution.py
@@ -239,39 +239,32 @@
         tail = voltages[:, frame * NFFT : (frame + 1) * NFFT]
         history[frame - frames] = lax.ppermute(tail, "ta", onward)
 
-    own, other, spectra = {}, {}, None
-
-    def swap(frame, spectra_or_owned):
-        owned = jnp.transpose(spectra_or_owned, (1, 0, 2))
-        own[frame] = owned
-        other[frame] = lax.ppermute(owned, "aa", across)
-
-    turned = {}
-    for frame in range(frames - 1, -1, -1):
-        at_needed = frame - (TAPS - 1)
-        if spectra is not None and at_needed < 0:
-            held = (history[at_needed], spectra)
-            if frame + 2 in turned:
-                history[at_needed], _, turned[frame + 2] = lax.optimization_barrier(
-                    held + (turned[frame + 2],))
-            else:
-                history[at_needed], _ = lax.optimization_barrier(held)
-        if frame + 2 in turned:
-            swap(frame + 2, turned.pop(frame + 2))
+    def turn(spectra):
+        return lax.all_to_all(
+            spectra.reshape(peers, CH // peers, 2 * signals), "ta",
+            split_axis=0, concat_axis=0, tiled=True)
+
+    spectra, turned, own, other = {}, {}, {}, {}
+    last = frames - 1
+    for frame in range(last, -1, -1):
+        oldest = frame - (TAPS - 1)
+        if frame < last and oldest < 0:
+            history[oldest], spectra[frame + 1] = lax.optimization_barrier(
+                (history[oldest], spectra[frame + 1]))
         pieces = []
         for tap in range(TAPS):
-            at = frame - (TAPS - 1) + tap
+            at = oldest + tap
             pieces.append((voltages, at) if at >= 0 else (history[at], 0))
-        spectra = channelize(pieces, pfb_window, signals)
-        if frame == 0:
-            for late in sorted(turned, reverse=True):
-                turned[late], spectra = lax.optimization_barrier((turned[late], spectra))
-                swap(late, turned.pop(late))
-        turned[frame] = lax.all_to_all(
-            spectra.reshape(peers, CH // peers, 2 * signals), "ta",
-            split_axis=0, concat_axis=0, tiled=True)
-    for late in sorted(turned, reverse=True):
-        swap(late, turned.pop(late))
+        spectra[frame] = channelize(pieces, pfb_window, signals)
+        if frame == last:
+            turned[last] = turn(spectra[last])
+    later = list(range(last - 1, -1, -1))
+    held = lax.optimization_barrier([spectra[f] for f in later])
+    for frame, value in zip(later, held):
+        turned[frame] = turn(value)
+    for frame in [last] + later:
+        own[frame] = jnp.transpose(turned[frame], (1, 0, 2))
+        other[frame] = lax.ppermute(own[frame], "aa", across)
 
     order = sorted(own)
     mine = [own[f] for f in order]

time: 226 us -> 229 us (1.013)
  blocking collectives: 0 us -> 58.1 us
  starting transfers between devices: 79.3 us -> 43.6 us
  waiting for transfers between devices: 72.3 us -> 53.5 us
    all_to_all x0 -> x1, blocking collectives: none -> 58.1 us  [turn(): lax.all_to_all(spectra.reshape(peers, CH // peers, 2 * signals), 'ta', sp...]
    all_to_all x3 -> x2, starting transfers between devices: 63.8 us -> 29 us  [turn(): lax.all_to_all(spectra.reshape(peers, CH // peers, 2 * signals), 'ta', sp...]
    all_to_all x3 -> x2, waiting for transfers between devices: 36.6 us -> 18.4 us  [turn(): lax.all_to_all(spectra.reshape(peers, CH // peers, 2 * signals), 'ta', sp...]
    optimization_barrier x2 -> x0, local copies, waits for them, and re-layouts: 2.39 us -> none  [the longest x1 1.81 us: per_device(): lax.optimization_barrier(held + (turned[frame + 2],))]
    all_to_all x1 -> x3, local copies, waits for them, and re-layouts: 1.81 us -> 4.2 us  [turn(): lax.all_to_all(spectra.reshape(peers, CH // peers, 2 * signals), 'ta', sp...]
  transfers between devices with their start and end apart: 9 -> 8, of which waited for: 5 -> 3; matrix products, arithmetic and copies ran while one was open for 2% -> 2% of each run, Pallas kernels for 21% -> 20%
where the time goes in v1:
time: 229 us; the launch traced here: 228 us
  Pallas kernels  62.3 us (27%)
  blocking collectives  58.1 us (25%)
  waiting for transfers between devices  53.5 us (23%)
  starting transfers between devices  43.6 us (19%)
  local copies, waits for them, and re-layouts  9.89 us (4%)
    all_to_all x1, blocking collectives, turn(): lax.all_to_all(spectra.reshape(peers, CH // peers, 2 * signals), 'ta', sp...  58.1 us
    pallas_call x3, Pallas kernels, channelize(): pl.pallas_call(functools.partial(channel_kernel, steps, signals), grid=(s...  35.6 us
    ppermute x3, waiting for transfers between devices, per_device(): other[frame] = lax.ppermute(own[frame], 'aa', across)  35.1 us
    all_to_all x2, starting transfers between devices, turn(): lax.all_to_all(spectra.reshape(peers, CH // peers, 2 * signals), 'ta', sp...  29 us
    pallas_call x2, Pallas kernels, correlate(): pl.pallas_call(functools.partial(correlate_kernel, len(mine), signals, bl...  26.8 us
    all_to_all x2, waiting for transfers between devices, turn(): lax.all_to_all(spectra.reshape(peers, CH // peers, 2 * signals), 'ta', sp...  18.4 us
    ppermute x3, starting transfers between devices, per_device(): history[frame - frames] = lax.ppermute(tail, 'ta', onward)  10.9 us
    slice x1, local copies, waits for them, and re-layouts, per_device(): tail = voltages[:, frame * NFFT:(frame + 1) * NFFT]  5.66 us
  transfers between devices with their start and end apart: 8, of which 3 were waited for; matrix products, arithmetic and copies ran while one was open for 2% of the time, Pallas kernels for 20%

profile of v1, /device:TPU:0, one launch (start us, length us, event | category | flops | bytes accessed | tf_op | source)
XLA Modules:
  0.0 227.5 jit_solution(7013486920686018152)
XLA Ops:
  0.0 5.7 %fusion = (bf16[128,8192]{1,0:T(8,128)(2,1)S(1)}, bf16[128,8192]{1,0:T(8,128)(2,1)}, bf16[128,8192]{1,0:T(8,128)(2,1)}) fusion(bf16[128,24576]{1,0:T(8,128)(2,1)} %refs_3_.5), kind=kLoop, calls=%fused_computation.3 | loop fusion | bytes 12582912 | tf_op jit(solution)/shard_map/slice | solution.py:239
  5.7 2.5 %collective-permute-start.2 = (bf16[128,8192]{1,0:T(8,128)(2,1)S(1)}, bf16[128,8192]{1,0:T(8,128)(2,1)S(1)}, u32[]{:S(2)}, u32[]{:S(2)}) collective-permute-start(bf16[128,8192]{1,0:T(8,128)(2,1)S(1)} %get-tuple-element.15), channel_id=1, source_target_pairs={{0,2},{2,4},{4,6},{6,8},{8,10},{10,12},{12,14},{14,16},{16,18},{18... | collective-permute-start | bytes 6291464 | tf_op jit(solution)/shard_map/ppermute | solution.py:240
  8.2 5.7 %collective-permute-start.1 = (bf16[128,8192]{1,0:T(8,128)(2,1)}, bf16[128,8192]{1,0:T(8,128)(2,1)}, u32[]{:S(2)}, u32[]{:S(2)}) collective-permute-start(bf16[128,8192]{1,0:T(8,128)(2,1)} %get-tuple-element.16), channel_id=1, source_target_pairs={{0,2},{2,4},{4,6},{6,8},{8,10},{10,12},{12,14},{14,16},{16,18},{18... | collective-permute-start | bytes 6291464 | tf_op jit(solution)/shard_map/ppermute | solution.py:240
  13.9 2.6 %collective-permute-start = (bf16[128,8192]{1,0:T(8,128)(2,1)}, bf16[128,8192]{1,0:T(8,128)(2,1)}, u32[]{:S(2)}, u32[]{:S(2)}) collective-permute-start(bf16[128,8192]{1,0:T(8,128)(2,1)} %get-tuple-element.17), channel_id=1, source_target_pairs={{0,2},{2,4},{4,6},{6,8},{8,10},{10,12},{12,14},{14,16},{16,18},{18... | collective-permute-start | bytes 6291464 | tf_op jit(solution)/shard_map/ppermute | solution.py:240
  16.5 0.0 collective-permute-done.2.refs_0_.refs_1_.refs_2_
  16.6 12.4 %shard_map.109 = bf16[2048,256]{1,0:T(8,128)(2,1)} custom-call(bf16[128,8192]{1,0:T(8,128)(2,1)S(1)} %collective-permute-done.2.refs_0_.refs_1_.refs_2_, bf16[128,24576]{1,0:T(8,128)(2,1)} %refs_3_.5, bf16[128,24576]{1,0:T(8,128)(2,1)} %refs_3_.5, bf16[128,24576]{1,0:T(8,128)(2,1)} %refs_3_.5, f32[4,8192]{1,0:T(4,128)S(1)} %copy-done.1, ...), custom_call_target="tpu_custom_call" | custom-call | flops 8000000000 | bytes 10000000 | tf_op jit(solution)/shard_map/pallas_call | solution.py:149
  29.0 23.9 %all-to-all-start.2 = ((bf16[16,128,256]{2,1,0:T(8,128)(2,1)}), bf16[16,128,256]{2,1,0:T(8,128)(2,1)}, u32[]{:S(2)}, u32[]{:S(2)}) async-start(bf16[16,128,256]{2,1,0:T(8,128)(2,1)} %bitcast.5), calls=%async_computation.2 | async-start | bytes 2097152 | tf_op jit(solution)/shard_map/all_to_all | solution.py:243
  52.9 0.0 copy-start.4
  52.9 0.0 copy-start.6
  53.0 11.9 %shard_map.110 = bf16[2048,256]{1,0:T(8,128)(2,1)} custom-call(bf16[128,8192]{1,0:T(8,128)(2,1)} %collective-permute-done.1.refs_0_.refs_1_, bf16[128,8192]{1,0:T(8,128)(2,1)S(1)} %collective-permute-done.2.refs_0_.refs_1_.refs_2_, bf16[128,24576]{1,0:T(8,128)(2,1)} %refs_3_.5, bf16[128,24576]{1,0:T(8,128)(2,1)} %refs_3_.5, f32[4,8192]{1,0:T(4,128)S(1)} %copy-done.1, ...), custom_call_target="tpu_custom_call" | custom-call | flops 8000000000 | bytes 10000000 | tf_op jit(solution)/shard_map/pallas_call | solution.py:149
  64.8 11.3 %shard_map.111 = bf16[2048,256]{1,0:T(8,128)(2,1)S(1)} custom-call(bf16[128,8192]{1,0:T(8,128)(2,1)} %collective-permute-done.refs_0_, bf16[128,8192]{1,0:T(8,128)(2,1)} %collective-permute-done.1.refs_0_.refs_1_, bf16[128,8192]{1,0:T(8,128)(2,1)} %copy-done, bf16[128,24576]{1,0:T(8,128)(2,1)} %refs_3_.5, f32[4,8192]{1,0:T(4,128)S(1)} %copy-done.1, ...), custom_call_target="tpu_custom_call" | custom-call | flops 8000000000 | bytes 10000000 | tf_op jit(solution)/shard_map/pallas_call | solution.py:149
  76.1 58.1 %all_to_all.15 = bf16[16,128,256]{2,1,0:T(8,128)(2,1)S(1)} all-to-all(bf16[16,128,256]{2,1,0:T(8,128)(2,1)S(1)} %bitcast.26), channel_id=1, replica_groups=mesh['ta'=16,'aa'=2] {'ta'}, dimensions={0} | all-to-all | bytes 2097152 | tf_op jit(solution)/shard_map/all_to_all | solution.py:243
  134.2 5.1 %all-to-all-start.1 = ((bf16[16,128,256]{2,1,0:T(8,128)(2,1)}), bf16[16,128,256]{2,1,0:T(8,128)(2,1)}, u32[]{:S(2)}, u32[]{:S(2)}) async-start(bf16[16,128,256]{2,1,0:T(8,128)(2,1)} %bitcast.3), calls=%async_computation.1 | async-start | bytes 2097152 | tf_op jit(solution)/shard_map/all_to_all | solution.py:243
  139.3 1.8 copy.22
  141.2 1.6 collective-permute-start.5
  142.7 0.6 copy.24
  143.3 0.6 collective-permute-start.3
  143.9 18.4 %all-to-all-done.1 = bf16[16,128,256]{2,1,0:T(8,128)(2,1)} async-done(((bf16[16,128,256]{2,1,0:T(8,128)(2,1)}), bf16[16,128,256]{2,1,0:T(8,128)(2,1)}, u32[]{:S(2)}, u32[]{:S(2)}) %all-to-all-start.1) | async-done | bytes 1048608 | tf_op jit(solution)/shard_map/all_to_all | solution.py:243
  162.3 1.8 copy.23
  164.1 1.6 collective-permute-start.4
  165.7 10.9 %shard_map.112.refs_7_ = f32[128,128,512]{2,1,0:T(8,128)} custom-call(s32[1]{0:T(128)} %bitcast.7.refs_0_, bf16[128,16,256]{2,1,0:T(8,128)(2,1)S(1)} %bitcast.19, bf16[128,16,256]{2,1,0:T(8,128)(2,1)S(1)} %bitcast.23, bf16[128,16,256]{2,1,0:T(8,128)(2,1)S(1)} %bitcast.15, bf16[128,16,256]{2,1,0:T(8,128)(2,1)S(1)} %bitcast.20, ...), custom_call_target="tpu_custom_call" | custom-call | flops 2000000000 | bytes 24000000 | tf_op jit(solution)/shard_map/pallas_call | solution.py:208
  176.6 13.3 %collective-permute-done.3.refs_4_ = bf16[128,16,256]{2,1,0:T(8,128)(2,1)} collective-permute-done((bf16[128,16,256]{2,1,0:T(8,128)(2,1)S(1)}, bf16[128,16,256]{2,1,0:T(8,128)(2,1)}, u32[]{:S(2)}, u32[]{:S(2)}) %collective-permute-start.3) | collective-permute-done | bytes 1048608 | tf_op jit(solution)/shard_map/ppermute | solution.py:267
  189.8 21.9 %collective-permute-done.4.refs_5_ = bf16[128,16,256]{2,1,0:T(8,128)(2,1)} collective-permute-done((bf16[128,16,256]{2,1,0:T(8,128)(2,1)S(1)}, bf16[128,16,256]{2,1,0:T(8,128)(2,1)}, u32[]{:S(2)}, u32[]{:S(2)}) %collective-permute-start.4) | collective-permute-done | bytes 1048608 | tf_op jit(solution)/shard_map/ppermute | solution.py:267
  211.7 15.9 %shard_map.113 = f32[128,128,512]{2,1,0:T(8,128)} custom-call(s32[1]{0:T(128)} %bitcast.refs_0_, bf16[128,16,256]{2,1,0:T(8,128)(2,1)S(1)} %bitcast.21, bf16[128,16,256]{2,1,0:T(8,128)(2,1)S(1)} %bitcast.25, bf16[128,16,256]{2,1,0:T(8,128)(2,1)S(1)} %bitcast.17, ...), custom_call_target="tpu_custom_call", output_to_operand_aliasing={{}: (7, {})} | custom-call | flops 2000000000 | bytes 24000000 | tf_op jit(solution)/shard_map/pallas_call | solution.py:208
  (16 shorter events, 0.0 us)
Async XLA Ops:
  0.0 16.5 %copy-start.2 = (bf16[256,512]{1,0:T(8,128)(2,1)S(1)}, bf16[256,512]{1,0:T(8,128)(2,1)}, u32[]{:S(2)}) copy-start(bf16[256,512]{1,0:T(8,128)(2,1)} %constant.14.clone.refs_7_) | copy-start | bytes 786436
  0.0 16.5 %copy-start.3 = (bf16[256,512]{1,0:T(8,128)(2,1)S(1)}, bf16[256,512]{1,0:T(8,128)(2,1)}, u32[]{:S(2)}) copy-start(bf16[256,512]{1,0:T(8,128)(2,1)} %constant.13.clone.refs_6_) | copy-start | bytes 786436
  0.0 16.5 %copy-start.5 = (f32[2,17,256]{2,1,0:T(8,128)S(1)}, f32[2,17,256]{2,1,0:T(8,128)}, u32[]{:S(2)}) copy-start(f32[2,17,256]{2,1,0:T(8,128)} %constant.12.clone.refs_5_) | copy-start | bytes 104452
  0.0 16.6 %copy-start.1 = (f32[4,8192]{1,0:T(4,128)S(1)}, f32[4,8192]{1,0:T(4,128)}, u32[]{:S(2)}) copy-start(f32[4,8192]{1,0:T(4,128)} %refs_4_.5) | copy-start | bytes 393220
  5.7 10.9 %collective-permute-start.2 = (bf16[128,8192]{1,0:T(8,128)(2,1)S(1)}, bf16[128,8192]{1,0:T(8,128)(2,1)S(1)}, u32[]{:S(2)}, u32[]{:S(2)}) collective-permute-start(bf16[128,8192]{1,0:T(8,128)(2,1)S(1)} %get-tuple-element.15), channel_id=1, source_target_pairs={{0,2},{2,4},{4,6},{6,8},{8,10},{10,12},{12,14},{14,16},{16,18},{18... | collective-permute-start | bytes 6291464 | tf_op jit(solution)/shard_map/ppermute | solution.py:240
  8.2 44.7 %collective-permute-start.1 = (bf16[128,8192]{1,0:T(8,128)(2,1)}, bf16[128,8192]{1,0:T(8,128)(2,1)}, u32[]{:S(2)}, u32[]{:S(2)}) collective-permute-start(bf16[128,8192]{1,0:T(8,128)(2,1)} %get-tuple-element.16), channel_id=1, source_target_pairs={{0,2},{2,4},{4,6},{6,8},{8,10},{10,12},{12,14},{14,16},{16,18},{18... | collective-permute-start | bytes 6291464 | tf_op jit(solution)/shard_map/ppermute | solution.py:240
  13.9 50.9 %collective-permute-start = (bf16[128,8192]{1,0:T(8,128)(2,1)}, bf16[128,8192]{1,0:T(8,128)(2,1)}, u32[]{:S(2)}, u32[]{:S(2)}) collective-permute-start(bf16[128,8192]{1,0:T(8,128)(2,1)} %get-tuple-element.17), channel_id=1, source_target_pairs={{0,2},{2,4},{4,6},{6,8},{8,10},{10,12},{12,14},{14,16},{16,18},{18... | collective-permute-start | bytes 6291464 | tf_op jit(solution)/shard_map/ppermute | solution.py:240
  16.6 36.4 %copy-start = (bf16[128,8192]{1,0:T(8,128)(2,1)}, bf16[128,8192]{1,0:T(8,128)(2,1)S(1)}, u32[]{:S(2)}) copy-start(bf16[128,8192]{1,0:T(8,128)(2,1)S(1)} %collective-permute-done.2.refs_0_.refs_1_.refs_2_) | copy-start | bytes 6291460
  29.0 47.1 %all-to-all-start.2 = ((bf16[16,128,256]{2,1,0:T(8,128)(2,1)}), bf16[16,128,256]{2,1,0:T(8,128)(2,1)}, u32[]{:S(2)}, u32[]{:S(2)}) async-start(bf16[16,128,256]{2,1,0:T(8,128)(2,1)} %bitcast.5), calls=%async_computation.2 | async-start | bytes 2097152 | tf_op jit(solution)/shard_map/all_to_all | solution.py:243
  52.9 11.9 %copy-start.4 = (bf16[256,512]{1,0:T(8,128)(2,1)S(1)}, bf16[256,512]{1,0:T(8,128)(2,1)}, u32[]{:S(2)}) copy-start(bf16[256,512]{1,0:T(8,128)(2,1)} %constant.13.clone.refs_6_) | copy-start | bytes 786436
  52.9 11.9 %copy-start.6 = (f32[2,17,256]{2,1,0:T(8,128)S(1)}, f32[2,17,256]{2,1,0:T(8,128)}, u32[]{:S(2)}) copy-start(f32[2,17,256]{2,1,0:T(8,128)} %constant.12.clone.refs_5_) | copy-start | bytes 104452
  134.2 28.0 %all-to-all-start.1 = ((bf16[16,128,256]{2,1,0:T(8,128)(2,1)}), bf16[16,128,256]{2,1,0:T(8,128)(2,1)}, u32[]{:S(2)}, u32[]{:S(2)}) async-start(bf16[16,128,256]{2,1,0:T(8,128)(2,1)} %bitcast.3), calls=%async_computation.1 | async-start | bytes 2097152 | tf_op jit(solution)/shard_map/all_to_all | solution.py:243
  141.2 35.4 %collective-permute-start.5 = (bf16[128,16,256]{2,1,0:T(8,128)(2,1)S(1)}, bf16[128,16,256]{2,1,0:T(8,128)(2,1)}, u32[]{:S(2)}, u32[]{:S(2)}) collective-permute-start(bf16[128,16,256]{2,1,0:T(8,128)(2,1)S(1)} %bitcast.14), channel_id=1, source_target_pairs={{0,1},{1,0},{2,3},{3,2},{4,5},{5,4},{6,7},{7,6},{8,9},{9,8},{10,11... | collective-permute-start | bytes 3145736 | tf_op jit(solution)/shard_map/ppermute | solution.py:267
  143.3 46.5 %collective-permute-start.3 = (bf16[128,16,256]{2,1,0:T(8,128)(2,1)S(1)}, bf16[128,16,256]{2,1,0:T(8,128)(2,1)}, u32[]{:S(2)}, u32[]{:S(2)}) collective-permute-start(bf16[128,16,256]{2,1,0:T(8,128)(2,1)S(1)} %bitcast.18), channel_id=1, source_target_pairs={{0,1},{1,0},{2,3},{3,2},{4,5},{5,4},{6,7},{7,6},{8,9},{9,8},{10,11... | collective-permute-start | bytes 3145736 | tf_op jit(solution)/shard_map/ppermute | solution.py:267
  164.1 47.6 %collective-permute-start.4 = (bf16[128,16,256]{2,1,0:T(8,128)(2,1)S(1)}, bf16[128,16,256]{2,1,0:T(8,128)(2,1)}, u32[]{:S(2)}, u32[]{:S(2)}) collective-permute-start(bf16[128,16,256]{2,1,0:T(8,128)(2,1)S(1)} %bitcast.22), channel_id=1, source_target_pairs={{0,1},{1,0},{2,3},{3,2},{4,5},{5,4},{6,7},{7,6},{8,9},{9,8},{10,11... | collective-permute-start | bytes 3145736 | tf_op jit(solution)/shard_map/ppermute | solution.py:267
